TPU v7x, 32 devices: a whole 2x2x4 slice. The times are simulated.
32 devices in a mesh: field: 2 (over x), expo: 8 (over z, y), sky: 2 (over core).
Axes of the slice: x: 2, y: 2, z: 4, core: 2. Of those that a mesh axis runs over, the one named last changes fastest.
Arguments:
- science: float32 [64, 64, 512], P(('field', 'expo'), 'sky'), parts along dimension 0, may hold values from -6 to 6
- inv_variance: float32 [64, 64, 512], P(('field', 'expo'), 'sky'), parts along dimension 0, may hold values from 0.25 to 4
- pixel_masks: int32 [64, 64, 512], P(('field', 'expo'), 'sky'), parts along dimension 0, may hold values 0 or 1
- point_spread: float32 [64, 5, 5], P(('field', 'expo')), parts along dimension 0, may hold values from 0.02 to 0.1
- tile_offset: int32 [8, 32], P(None, 'expo'), may hold values from 0 to 1
- column_shift: int32 [8, 32], P(None, 'expo'), may hold values from -128 to 128
- trail_kernel: float32 [8, 3, 3], P('expo'), may hold values from 0.1 to 1
Outputs:
- likelihood: float32 [16, 64, 512], P(('field', 'expo'), 'sky'), parts along dimension 0
There are 2 independent parts, one for each index of `field`. A program takes and returns all parts, laid end to end along the dimension named above; an argument that names none is the same for every part. Nothing has to cross between parts.
All inputs are finite; a program needn't handle non-finite values. No bound on the sum of `pixel_masks` on one device may be relied on, other than what follows from the above.
Results may differ from a plain program's by a relative error of at most 0.0003.
Values sent between devices are 32-bit elements; how exact they have to be, the bound alone decides.
No kernel may reach another device: no remote copies, remote signals or barrier semaphores. Data moves between devices by JAX's collectives and lax.ppermute only.
A program may use at most 128 MiB of HBM per device.

v0:
```python
import functools

import jax
import jax.numpy as jnp
from jax import lax
from jax.experimental import pallas as pl
from jax.experimental.pallas import tpu as pltpu
from jax.sharding import PartitionSpec as P


MAX_SHIFT = 128
LANES = 128
SUB = 8


def lane_shifted(pieces, lane, offset):
    if offset == 0:
        return pieces
    count = len(pieces)
    rolled = [pltpu.roll(piece, (-offset) % LANES, 1) for piece in pieces]
    out = []
    for c in range(count):
        near = rolled[c]
        if offset > 0:
            far = rolled[c + 1] if c + 1 < count else jnp.zeros_like(near)
            out.append(jnp.where(lane < LANES - offset, near, far))
        else:
            far = rolled[c - 1] if c > 0 else jnp.zeros_like(near)
            out.append(jnp.where(lane >= -offset, near, far))
    return out


def filter_rows(load, taps, row_taps, chunks, lane):
    half = row_taps // 2
    columns = [[None] * chunks for _ in range(row_taps)]
    for c in range(chunks):
        rows = [load(a, c) for a in range(row_taps)]
        for b in range(row_taps):
            total = rows[0] * taps[0][b]
            for a in range(1, row_taps):
                total = total + rows[a] * taps[a][b]
            columns[b][c] = total
    result = columns[half]
    for b in range(row_taps):
        if b != half:
            moved = lane_shifted(columns[b], lane, b - half)
            result = [x + y for x, y in zip(result, moved)]
    return result


def filter_groups(image, wide, taps_of, first, count, exposures, chunks, taps, lane):
    half = taps // 2
    for e in range(exposures):
        for k in range(2):
            scale = taps_of(e, k)
            for g in range(count):
                row = pl.multiple_of((first + g) * SUB, SUB)

                def load(a, c):
                    return image[k, e, c, pl.ds(row + (SUB + a - half), SUB), :]

                result = filter_rows(load, scale, taps, chunks, lane)
                for c in range(chunks):
                    wide[e, k, 1 + c, pl.ds(row, SUB), :] = result[c]


def taps_in(spread_ref, taps):
    def taps_of(e, k):
        scale = [[spread_ref[a, e, b] for b in range(taps)] for a in range(taps)]
        return scale if k == 0 else [[x * x for x in line] for line in scale]

    return taps_of


def vectors_in(load, taps):
    return lambda e, k: [[load(e, k, a * taps + b) for b in range(taps)] for a in range(taps)]


def near_kernel(spread_ref, own_ref, image, wide, spread_out, *, rows, chunks, taps):
    exposures = own_ref.shape[1]
    sky = lax.axis_index("sky")
    lane = lax.broadcasted_iota(jnp.int32, (SUB, LANES), 1)
    zero = jnp.zeros((SUB, LANES), jnp.float32)
    base = pl.multiple_of(SUB + rows * sky, SUB)
    for k in range(2):
        for e in range(exposures):
            for c in range(chunks):
                image[k, e, c, 0:SUB, :] = zero
                image[k, e, c, SUB + 2 * rows :, :] = zero
                image[k, e, c, pl.ds(base, rows), :] = own_ref[k, e, :, c * LANES : (c + 1) * LANES]
    inside = rows // SUB - 1
    first = (2 * (rows // SUB) - inside) * sky
    scalars = taps_in(spread_ref, taps)

    def taps_of(e, k):
        scale = [[zero + x for x in line] for line in scalars(e, k)]
        for a in range(taps):
            for b in range(taps):
                spread_out[e, k, a * taps + b] = scale[a][b]
        return scale

    filter_groups(image, wide, taps_of, first, inside, exposures, chunks, taps, lane)
    blank = jnp.zeros((2 * rows, LANES), jnp.float32)
    for e in range(exposures):
        for k in range(2):
            for c in (0, chunks + 1, chunks + 2):
                wide[e, k, c] = blank


def stack_velocity(out, p, v, wide, edge, offset_ref, shift_ref, sky, rows, chunks, lane):
    exposures = wide.shape[0]
    totals = [None, None]
    edges = None
    groups = rows // SUB
    for e in range(exposures):
        tile = lax.rem(sky + offset_ref[e, v], 2)
        start = MAX_SHIFT - shift_ref[e, v]
        skip = lax.div(start, LANES)
        turn = lax.rem(start, LANES)
        back = lax.rem(LANES - turn, LANES)
        keep = lane < LANES - turn
        base = pl.multiple_of(tile * rows, SUB)
        for k in range(2):
            moved = [
                [
                    pltpu.roll(wide[e, k, skip + c, pl.ds(pl.multiple_of(base + g * SUB, SUB), SUB), :], back, 1)
                    for g in range(groups)
                ]
                for c in range(chunks + 1)
            ]
            picked = [
                [jnp.where(keep, moved[c][g], moved[c + 1][g]) for g in range(groups)] for c in range(chunks)
            ]
            if totals[k] is None:
                totals[k] = picked
            else:
                totals[k] = [[x + y for x, y in zip(p0, p1)] for p0, p1 in zip(totals[k], picked)]
        moved = [pltpu.roll(edge[e, 1 - tile, skip + c], back, 1) for c in range(chunks + 1)]
        picked = [jnp.where(keep, moved[c], moved[c + 1]) for c in range(chunks)]
        edges = picked if edges is None else [x + y for x, y in zip(edges, picked)]
    for k in range(2):
        for c in range(chunks):
            for g in range(groups):
                row = (k * chunks + c) * rows + g * SUB
                out[p, row : row + SUB, :] = totals[k][c][g]
    for c in range(chunks):
        row = 2 * chunks * rows + 2 * c
        out[p, row : row + 2, :] = edges[c][0:2, :]


def stack_targets(outs, hops, wide, edge, offset_ref, shift_ref, sky, rows, chunks, lane):
    me = lax.axis_index("expo")
    for out, hop in zip(outs, hops):
        owner = jnp.bitwise_xor(me, jnp.where(sky == 0, hop, turned(hop)))
        for p in range(out.shape[0]):
            stack_velocity(
                out, p, owner * out.shape[0] + p, wide, edge, offset_ref, shift_ref, sky, rows, chunks, lane
            )


def turned(hop):
    return (hop & ~3) | ((hop & 1) << 1) | ((hop >> 1) & 1)


def far_kernel(
    spread_ref, offset_from, shift_from, other_ref, image_in, wide_in, image, wide, edge, *rest,
    hops, rows, chunks, taps,
):
    outs = rest[: len(hops)]
    offset_ref, shift_ref, offset_sem, shift_sem = rest[len(hops):]
    offset_copy = pltpu.make_async_copy(offset_from, offset_ref, offset_sem)
    shift_copy = pltpu.make_async_copy(shift_from, shift_ref, shift_sem)
    offset_copy.start()
    shift_copy.start()
    exposures = other_ref.shape[1]
    sky = lax.axis_index("sky")
    lane = lax.broadcasted_iota(jnp.int32, (SUB, LANES), 1)
    zero = jnp.zeros((SUB, LANES), jnp.float32)
    base = pl.multiple_of(SUB + rows * (1 - sky), SUB)
    for k in range(2):
        for e in range(exposures):
            for c in range(chunks):
                image[k, e, c, pl.ds(base, rows), :] = other_ref[k, e, :, c * LANES : (c + 1) * LANES]
    inside = rows // SUB - 1
    filter_groups(
        image, wide, vectors_in(lambda e, k, i: spread_ref[e, k, i], taps), inside * (1 - sky),
        2 * (rows // SUB) - inside, exposures, chunks, taps, lane,
    )
    at_row = (rows - 1) * sky
    for e in range(exposures):
        for t in range(2):
            for c in (0, chunks + 1, chunks + 2):
                edge[e, t, c] = zero
            for k in range(2):
                for c in range(chunks):
                    edge[e, t, 1 + c, k : k + 1, :] = wide[e, k, 1 + c, pl.ds(rows * t + at_row, 1), :]
    offset_copy.wait()
    shift_copy.wait()
    stack_targets(outs, hops, wide, edge, offset_ref, shift_ref, sky, rows, chunks, lane)


def rest_kernel(offset_ref, shift_ref, wide, edge, *outs, hops, rows, chunks):
    sky = lax.axis_index("sky")
    lane = lax.broadcasted_iota(jnp.int32, (SUB, LANES), 1)
    stack_targets(outs, hops, wide, edge, offset_ref, shift_ref, sky, rows, chunks, lane)


def last_kernel(offset_ref, shift_ref, trail_ref, wide, edge, trail_out, *outs, hops, rows, chunks):
    sky = lax.axis_index("sky")
    lane = lax.broadcasted_iota(jnp.int32, (SUB, LANES), 1)
    taps = trail_ref.shape[0]
    for p in range(trail_ref.shape[1]):
        for a in range(taps):
            for b in range(taps):
                value = jnp.zeros((SUB, LANES), jnp.float32) + trail_ref[a, p, b]
                trail_out[p, 0, a * taps + b] = value
                trail_out[p, 1, a * taps + b] = value * value
    stack_targets(outs, hops, wide, edge, offset_ref, shift_ref, sky, rows, chunks, lane)


def trail_kernel_body(trail_ref, *rest, rows, chunks, taps):
    parts = rest[:-2]
    out, image = rest[-2:]
    sky = lax.axis_index("sky")
    lane = lax.broadcasted_iota(jnp.int32, (SUB, LANES), 1)
    zero = jnp.zeros((SUB, LANES), jnp.float32)
    half = taps // 2
    groups = rows // SUB
    for p in range(out.shape[0]):
        def total(row, count):
            value = parts[0][p, row : row + count, :]
            for part in parts[1:]:
                value = value + part[p, row : row + count, :]
            return value

        results = []
        edges = total(2 * chunks * rows, 2 * chunks)
        for k in range(2):
            for c in range(chunks):
                image[c, 0:SUB, :] = zero
                image[c, SUB + rows :, :] = zero
                for g in range(groups):
                    image[c, SUB + g * SUB : SUB + (g + 1) * SUB, :] = total((k * chunks + c) * rows + g * SUB, SUB)
                at = jnp.where(sky == 0, SUB + rows, SUB - 1)
                image[c, pl.ds(at, 1), :] = edges[2 * c + k : 2 * c + k + 1, :]
            scale = [[trail_ref[p, k, a * taps + b] for b in range(taps)] for a in range(taps)]
            kind = []
            for g in range(groups):
                def load(a, c):
                    return image[c, SUB + g * SUB + a - half : SUB + g * SUB + a - half + SUB, :]

                kind.append(filter_rows(load, scale, taps, chunks, lane))
            results.append(kind)
        for g in range(groups):
            for c in range(chunks):
                value = results[0][g][c] / jnp.sqrt(results[1][g][c] + 1.0)
                out[p, g * SUB : (g + 1) * SUB, c * LANES : (c + 1) * LANES] = value


SMEM = pl.BlockSpec(memory_space=pltpu.SMEM)
VMEM = pl.BlockSpec(memory_space=pltpu.VMEM)
ANY = pl.BlockSpec(memory_space=pl.ANY)


def call(body, outputs, inputs, scratch=(), aliases={}, megabytes=8):
    return pl.pallas_call(
        body,
        out_shape=[jax.ShapeDtypeStruct(shape, jnp.float32) for shape in outputs],
        in_specs=[spec for spec, _ in inputs],
        out_specs=[VMEM] * len(outputs),
        scratch_shapes=scratch,
        input_output_aliases=aliases,
        compiler_params=pltpu.CompilerParams(vmem_limit_bytes=megabytes * 1024 * 1024),
    )(*[value for _, value in inputs])


def steps(
    science, inv_variance, pixel_masks, point_spread, tile_offset, column_shift, trail_kernel
):
    exposures, rows, width = science.shape
    chunks = width // LANES
    taps = point_spread.shape[-1]
    trail_taps = trail_kernel.shape[-1]
    count = lax.axis_size("expo")
    per = tile_offset.shape[0] // count

    weighted = inv_variance * pixel_masks.astype(jnp.float32)
    own = jnp.stack([science * weighted, weighted])
    other = lax.ppermute(own, "sky", [(0, 1), (1, 0)])

    spread = (SMEM, jnp.transpose(point_spread, (1, 0, 2)))
    offsets = (SMEM, tile_offset.T)
    shifts = (SMEM, column_shift.T)
    image_shape = (2, exposures, chunks, 2 * rows + 2 * SUB, LANES)
    wide_shape = (exposures, 2, chunks + 3, 2 * rows, LANES)
    edge_shape = (exposures, 2, chunks + 3, SUB, LANES)
    part = (per, 2 * chunks * rows + 2 * chunks, LANES)

    spread_shape = (exposures, 2, taps * taps, SUB, LANES)
    image, wide, spread = call(
        functools.partial(near_kernel, rows=rows, chunks=chunks, taps=taps),
        [image_shape, wide_shape, spread_shape], [spread, (VMEM, own)],
    )
    early, middle, late = stacking_order(count)
    results = call(
        functools.partial(far_kernel, hops=early, rows=rows, chunks=chunks, taps=taps),
        [image_shape, wide_shape, edge_shape] + [part] * len(early),
        [
            (VMEM, spread), (ANY, offsets[1]), (ANY, shifts[1]), (VMEM, other), (VMEM, image), (VMEM, wide),
        ],
        scratch=[
            pltpu.SMEM(offsets[1].shape, jnp.int32), pltpu.SMEM(shifts[1].shape, jnp.int32),
            pltpu.SemaphoreType.DMA(()), pltpu.SemaphoreType.DMA(()),
        ],
        aliases={4: 0, 5: 1},
    )
    wide, edge = results[1:3]
    parts = dict(zip(early, results[3:]))
    results = call(
        functools.partial(rest_kernel, hops=middle, rows=rows, chunks=chunks),
        [part] * len(middle), [offsets, shifts, (VMEM, wide), (VMEM, edge)],
    )
    parts.update(zip(middle, results))
    results = call(
        functools.partial(last_kernel, hops=late, rows=rows, chunks=chunks),
        [(per, 2, trail_taps * trail_taps, SUB, LANES)] + [part] * len(late),
        [offsets, shifts, (SMEM, jnp.transpose(trail_kernel, (1, 0, 2))), (VMEM, wide), (VMEM, edge)],
    )
    trail = results[0]
    parts.update(zip(late, results[1:]))

    bit = 1
    while bit < count:
        pairs = [
            (2 * i + core, 2 * (i ^ (turned(bit) if core else bit)) + core)
            for i in range(count) for core in range(2)
        ]
        for hop in range(count - bit, 0, -2 * bit):
            moved = lax.ppermute(parts[hop], ("expo", "sky"), pairs)
            parts[hop - bit] = parts[hop - bit] + moved
        bit *= 2
    total = parts[0]

    return call(
        functools.partial(trail_kernel_body, rows=rows, chunks=chunks, taps=trail_taps),
        [(per, rows, width)],
        [(VMEM, trail), (VMEM, total)],
        scratch=[pltpu.VMEM((chunks, rows + 2 * SUB, LANES), jnp.float32)],
    )[0]


def stacking_order(count):
    early = [hop for hop in (count - 1, count - 3) if hop > 0]
    middle = [hop for hop in (count - 2, count - 5) if hop > 0 and hop not in early]
    return early, middle, [hop for hop in range(count - 1, -1, -1) if hop not in early + middle]


def solution(mesh):
    return jax.shard_map(
        steps,
        mesh=mesh,
        in_specs=(
            P(("field", "expo"), "sky", None),
            P(("field", "expo"), "sky", None),
            P(("field", "expo"), "sky", None),
            P(("field", "expo"), None, None),
            P(None, "expo"),
            P(None, "expo"),
            P("expo", None, None),
        ),
        out_specs=P(("field", "expo"), "sky", None),
        check_vma=False,
    )
```

profile of v0, /device:TPU:0, one launch (start us, length us, event | category | flops | bytes accessed | tf_op | source)
XLA Modules:
  0.0 27.3 jit_solution(2610444789826070863)
XLA Ops:
  0.0 0.0 copy-start.2
  0.0 0.0 copy-start.1
  0.0 0.0 copy-start
  0.0 1.2 %multiply_bitcast_fusion = (f32[1,4,32,512]{3,2,1,0:T(8,128)S(1)}, f32[1,4,32,512]{3,2,1,0:T(8,128)S(1)}) fusion(f32[4,32,512]{2,1,0:T(8,128)} %param.7, f32[4,32,512]{2,1,0:T(8,128)} %param.8, s32[4,32,512]{2,1,0:T(8,128)} %param.9), kind=kLoop, calls=%fused_computation.1 | loop fusion | flops 196608 | bytes 1310720 | tf_op jit(solution)/shard_map/stack | solution.py:288
  1.3 0.6 %collective-permute-start = (f32[2,4,32,512]{3,2,1,0:T(8,128)S(1)}, f32[2,4,32,512]{3,2,1,0:T(8,128)S(1)}, u32[]{:S(2)}, u32[]{:S(2)}) collective-permute-start(f32[2,4,32,512]{3,2,1,0:T(8,128)S(1)} %pad_maximum_fusion.own_ref), channel_id=1, source_target_pairs={{0,1},{1,0},{2,3},{3,2},{4,5},{5,4},{6,7},{7,6},{8,9},{9,8},{10,11... | collective-permute-start | bytes 1572872 | tf_op jit(solution)/shard_map/ppermute | solution.py:289
  1.8 0.0 copy-done.2
  1.8 1.5 %shard_map.73 = (f32[2,4,4,80,128]{4,3,2,1,0:T(8,128)S(1)}, f32[4,2,7,64,128]{4,3,2,1,0:T(8,128)S(1)}, f32[4,2,25,8,128]{4,3,2,1,0:T(8,128)S(1)}) custom-call(f32[5,4,5]{2,1,0:T(4,128)S(1)} %bitcast.14, f32[2,4,32,512]{3,2,1,0:T(8,128)S(1)} %pad_maximum_fusion.own_ref), custom_call_target="tpu_custom_call" | custom-call | tf_op jit(solution)/shard_map/pallas_call | solution.py:266
  3.4 0.0 collective-permute-done.other_ref
  3.4 0.0 copy-done.1
  3.4 0.0 copy-done
  3.4 2.3 %shard_map.74 = (f32[2,4,4,80,128]{4,3,2,1,0:T(8,128)S(1)}, f32[4,2,7,64,128]{4,3,2,1,0:T(8,128)S(1)}, f32[4,2,7,8,128]{4,3,2,1,0:T(8,128)S(1)}, f32[1,264,128]{2,1,0:T(8,128)S(1)}, f32[1,264,128]{2,1,0:T(8,128)S(1)}) custom-call(f32[4,2,25,8,128]{4,3,2,1,0:T(8,128)S(1)} %get-tuple-element.19.spread_ref, ...), custom_call_target="tpu_custom_call", output_to_operand_aliasing={{0}: (4, {}), {1}: (5, {})} | custom-call | tf_op jit(solution)/shard_map/pallas_call | solution.py:266
  5.7 0.0 copy-start.3
  5.7 2.9 %collective-permute-start.5 = (f32[1,264,128]{2,1,0:T(8,128)S(1)}, f32[1,264,128]{2,1,0:T(8,128)S(1)}, u32[]{:S(2)}, u32[]{:S(2)}) collective-permute-start(f32[1,264,128]{2,1,0:T(8,128)S(1)} %get-tuple-element.32), channel_id=1, source_target_pairs={{0,2},{1,5},{2,0},{3,7},{4,6},{5,1},{6,4},{7,3},{8,10},{9,13},{10,... | collective-permute-start | bytes 405512 | tf_op jit(solution)/shard_map/ppermute | solution.py:339
  8.6 1.1 %shard_map.76 = (f32[1,264,128]{2,1,0:T(8,128)S(1)}, f32[1,264,128]{2,1,0:T(8,128)S(1)}) custom-call(s32[4,8]{1,0:T(4,128)S(1)} %bitcast.9, s32[4,8]{1,0:T(4,128)S(1)} %bitcast.12, f32[4,2,7,64,128]{4,3,2,1,0:T(8,128)S(1)} %get-tuple-element.22.wide, f32[4,2,7,8,128]{4,3,2,1,0:T(8,128)S(1)} %get-tuple-element.23.edge), custom_call_target="tpu_custom_call" | custom-call | tf_op jit(solution)/shard_map/pallas_call | solution.py:266
  9.7 0.1 collective-permute-start.2
  9.7 2.0 %collective-permute-start.4 = (f32[1,264,128]{2,1,0:T(8,128)S(1)}, f32[1,264,128]{2,1,0:T(8,128)S(1)}, u32[]{:S(2)}, u32[]{:S(2)}) collective-permute-start(f32[1,264,128]{2,1,0:T(8,128)S(1)} %get-tuple-element.30), channel_id=1, source_target_pairs={{0,2},{1,5},{2,0},{3,7},{4,6},{5,1},{6,4},{7,3},{8,10},{9,13},{10,... | collective-permute-start | bytes 405512 | tf_op jit(solution)/shard_map/ppermute | solution.py:339
  11.7 0.0 collective-permute-done.5
  11.8 2.0 %collective-permute-start.6 = (f32[1,264,128]{2,1,0:T(8,128)S(1)}, f32[1,264,128]{2,1,0:T(8,128)S(1)}, u32[]{:S(2)}, u32[]{:S(2)}) collective-permute-start(f32[1,264,128]{2,1,0:T(8,128)S(1)} %add.25), channel_id=1, source_target_pairs={{0,4},{1,3},{2,6},{3,1},{4,0},{5,7},{6,2},{7,5},{8,12},{9,11},{10,... | collective-permute-start | bytes 405512 | tf_op jit(solution)/shard_map/ppermute | solution.py:339
  13.7 0.0 copy-done.3
  13.7 1.5 %shard_map.75 = (f32[1,2,9,8,128]{4,3,2,1,0:T(8,128)S(1)}, f32[1,264,128]{2,1,0:T(8,128)S(1)}, f32[1,264,128]{2,1,0:T(8,128)S(1)}, f32[1,264,128]{2,1,0:T(8,128)S(1)}, f32[1,264,128]{2,1,0:T(8,128)S(1)}) custom-call(s32[4,8]{1,0:T(4,128)S(1)} %bitcast.10, s32[4,8]{1,0:T(4,128)S(1)} %bitcast.13, f32[3,1,3]{2,1,0:T(1,128)S(1)} %bitcast.15, ...), custom_call_target="tpu_custom_call" | custom-call | tf_op jit(solution)/shard_map/pallas_call | solution.py:266
  15.2 1.6 %collective-permute-start.1 = (f32[1,264,128]{2,1,0:T(8,128)S(1)}, f32[1,264,128]{2,1,0:T(8,128)S(1)}, u32[]{:S(2)}, u32[]{:S(2)}) collective-permute-start(f32[1,264,128]{2,1,0:T(8,128)S(1)} %get-tuple-element.26), channel_id=1, source_target_pairs={{0,2},{1,5},{2,0},{3,7},{4,6},{5,1},{6,4},{7,3},{8,10},{9,13},{10,... | collective-permute-start | bytes 405512 | tf_op jit(solution)/shard_map/ppermute | solution.py:339
  16.8 0.0 collective-permute-done.2
  16.8 0.5 %collective-permute-start.3 = (f32[1,264,128]{2,1,0:T(8,128)S(1)}, f32[1,264,128]{2,1,0:T(8,128)S(1)}, u32[]{:S(2)}, u32[]{:S(2)}) collective-permute-start(f32[1,264,128]{2,1,0:T(8,128)S(1)} %add.22), channel_id=1, source_target_pairs={{0,4},{1,3},{2,6},{3,1},{4,0},{5,7},{6,2},{7,5},{8,12},{9,11},{10,... | collective-permute-start | bytes 405512 | tf_op jit(solution)/shard_map/ppermute | solution.py:339
  17.3 0.3 %collective-permute-done.4 = f32[1,264,128]{2,1,0:T(8,128)S(1)} collective-permute-done((f32[1,264,128]{2,1,0:T(8,128)S(1)}, f32[1,264,128]{2,1,0:T(8,128)S(1)}, u32[]{:S(2)}, u32[]{:S(2)}) %collective-permute-start.4) | collective-permute-done | bytes 135200 | tf_op jit(solution)/shard_map/ppermute | solution.py:339
  17.6 0.0 collective-permute-done.6
  17.7 2.7 %collective-permute-start.7 = (f32[1,264,128]{2,1,0:T(8,128)S(1)}, f32[1,264,128]{2,1,0:T(8,128)S(1)}, u32[]{:S(2)}, u32[]{:S(2)}) collective-permute-start(f32[1,264,128]{2,1,0:T(8,128)S(1)} %add_add_fusion), channel_id=1, source_target_pairs={{0,8},{1,9},{2,10},{3,11},{4,12},{5,13},{6,14},{7,15},{8,0},{9,1},... | collective-permute-start | bytes 405512 | tf_op jit(solution)/shard_map/ppermute | solution.py:339
  20.3 0.8 %collective-permute-done.1 = f32[1,264,128]{2,1,0:T(8,128)S(1)} collective-permute-done((f32[1,264,128]{2,1,0:T(8,128)S(1)}, f32[1,264,128]{2,1,0:T(8,128)S(1)}, u32[]{:S(2)}, u32[]{:S(2)}) %collective-permute-start.1) | collective-permute-done | bytes 135200 | tf_op jit(solution)/shard_map/ppermute | solution.py:339
  21.1 2.3 %collective-permute-done.3 = f32[1,264,128]{2,1,0:T(8,128)S(1)} collective-permute-done((f32[1,264,128]{2,1,0:T(8,128)S(1)}, f32[1,264,128]{2,1,0:T(8,128)S(1)}, u32[]{:S(2)}, u32[]{:S(2)}) %collective-permute-start.3) | collective-permute-done | bytes 135200 | tf_op jit(solution)/shard_map/ppermute | solution.py:339
  23.4 3.1 %collective-permute-done.7 = f32[1,264,128]{2,1,0:T(8,128)S(1)} collective-permute-done((f32[1,264,128]{2,1,0:T(8,128)S(1)}, f32[1,264,128]{2,1,0:T(8,128)S(1)}, u32[]{:S(2)}, u32[]{:S(2)}) %collective-permute-start.7) | collective-permute-done | bytes 135200 | tf_op jit(solution)/shard_map/ppermute | solution.py:339
  26.5 0.8 %shard_map.77 = f32[1,32,512]{2,1,0:T(8,128)} custom-call(f32[1,2,9,8,128]{4,3,2,1,0:T(8,128)S(1)} %get-tuple-element.24.trail_ref, f32[1,264,128]{2,1,0:T(8,128)S(1)} %add_add_fusion.1.rest_0_), custom_call_target="tpu_custom_call" | custom-call | tf_op jit(solution)/shard_map/pallas_call | solution.py:266
  (5 shorter events, 0.1 us)
Async XLA Ops:
  0.0 1.8 %copy-start.2 = (f32[4,5,5]{2,0,1:T(4,128)S(1)}, f32[4,5,5]{2,0,1:T(4,128)}, u32[]{:S(2)}) copy-start(f32[4,5,5]{2,0,1:T(4,128)} %param.10) | copy-start | bytes 1204
  0.0 3.4 %copy-start.1 = (s32[8,4]{0,1:T(4,128)S(1)}, s32[8,4]{0,1:T(4,128)}, u32[]{:S(2)}) copy-start(s32[8,4]{0,1:T(4,128)} %param.12) | copy-start | bytes 388
  0.0 3.4 %copy-start = (s32[8,4]{0,1:T(4,128)S(1)}, s32[8,4]{0,1:T(4,128)}, u32[]{:S(2)}) copy-start(s32[8,4]{0,1:T(4,128)} %param.11) | copy-start | bytes 388
  1.3 2.1 %collective-permute-start = (f32[2,4,32,512]{3,2,1,0:T(8,128)S(1)}, f32[2,4,32,512]{3,2,1,0:T(8,128)S(1)}, u32[]{:S(2)}, u32[]{:S(2)}) collective-permute-start(f32[2,4,32,512]{3,2,1,0:T(8,128)S(1)} %pad_maximum_fusion.own_ref), channel_id=1, source_target_pairs={{0,1},{1,0},{2,3},{3,2},{4,5},{5,4},{6,7},{7,6},{8,9},{9,8},{10,11... | collective-permute-start | bytes 1572872 | tf_op jit(solution)/shard_map/ppermute | solution.py:289
  5.7 8.1 %copy-start.3 = (f32[1,3,3]{2,0,1:T(1,128)S(1)}, f32[1,3,3]{2,0,1:T(1,128)}, u32[]{:S(2)}) copy-start(f32[1,3,3]{2,0,1:T(1,128)} %param.13) | copy-start | bytes 112
  5.7 6.1 %collective-permute-start.5 = (f32[1,264,128]{2,1,0:T(8,128)S(1)}, f32[1,264,128]{2,1,0:T(8,128)S(1)}, u32[]{:S(2)}, u32[]{:S(2)}) collective-permute-start(f32[1,264,128]{2,1,0:T(8,128)S(1)} %get-tuple-element.32), channel_id=1, source_target_pairs={{0,2},{1,5},{2,0},{3,7},{4,6},{5,1},{6,4},{7,3},{8,10},{9,13},{10,... | collective-permute-start | bytes 405512 | tf_op jit(solution)/shard_map/ppermute | solution.py:339
  9.7 7.1 %collective-permute-start.2 = (f32[1,264,128]{2,1,0:T(8,128)S(1)}, f32[1,264,128]{2,1,0:T(8,128)S(1)}, u32[]{:S(2)}, u32[]{:S(2)}) collective-permute-start(f32[1,264,128]{2,1,0:T(8,128)S(1)} %get-tuple-element.28), channel_id=1, source_target_pairs={{0,2},{1,5},{2,0},{3,7},{4,6},{5,1},{6,4},{7,3},{8,10},{9,13},{10,... | collective-permute-start | bytes 405512 | tf_op jit(solution)/shard_map/ppermute | solution.py:339
  9.7 7.9 %collective-permute-start.4 = (f32[1,264,128]{2,1,0:T(8,128)S(1)}, f32[1,264,128]{2,1,0:T(8,128)S(1)}, u32[]{:S(2)}, u32[]{:S(2)}) collective-permute-start(f32[1,264,128]{2,1,0:T(8,128)S(1)} %get-tuple-element.30), channel_id=1, source_target_pairs={{0,2},{1,5},{2,0},{3,7},{4,6},{5,1},{6,4},{7,3},{8,10},{9,13},{10,... | collective-permute-start | bytes 405512 | tf_op jit(solution)/shard_map/ppermute | solution.py:339
  11.8 5.9 %collective-permute-start.6 = (f32[1,264,128]{2,1,0:T(8,128)S(1)}, f32[1,264,128]{2,1,0:T(8,128)S(1)}, u32[]{:S(2)}, u32[]{:S(2)}) collective-permute-start(f32[1,264,128]{2,1,0:T(8,128)S(1)} %add.25), channel_id=1, source_target_pairs={{0,4},{1,3},{2,6},{3,1},{4,0},{5,7},{6,2},{7,5},{8,12},{9,11},{10,... | collective-permute-start | bytes 405512 | tf_op jit(solution)/shard_map/ppermute | solution.py:339
  15.2 5.9 %collective-permute-start.1 = (f32[1,264,128]{2,1,0:T(8,128)S(1)}, f32[1,264,128]{2,1,0:T(8,128)S(1)}, u32[]{:S(2)}, u32[]{:S(2)}) collective-permute-start(f32[1,264,128]{2,1,0:T(8,128)S(1)} %get-tuple-element.26), channel_id=1, source_target_pairs={{0,2},{1,5},{2,0},{3,7},{4,6},{5,1},{6,4},{7,3},{8,10},{9,13},{10,... | collective-permute-start | bytes 405512 | tf_op jit(solution)/shard_map/ppermute | solution.py:339
  16.8 6.5 %collective-permute-start.3 = (f32[1,264,128]{2,1,0:T(8,128)S(1)}, f32[1,264,128]{2,1,0:T(8,128)S(1)}, u32[]{:S(2)}, u32[]{:S(2)}) collective-permute-start(f32[1,264,128]{2,1,0:T(8,128)S(1)} %add.22), channel_id=1, source_target_pairs={{0,4},{1,3},{2,6},{3,1},{4,0},{5,7},{6,2},{7,5},{8,12},{9,11},{10,... | collective-permute-start | bytes 405512 | tf_op jit(solution)/shard_map/ppermute | solution.py:339
  17.7 8.8 %collective-permute-start.7 = (f32[1,264,128]{2,1,0:T(8,128)S(1)}, f32[1,264,128]{2,1,0:T(8,128)S(1)}, u32[]{:S(2)}, u32[]{:S(2)}) collective-permute-start(f32[1,264,128]{2,1,0:T(8,128)S(1)} %add_add_fusion), channel_id=1, source_target_pairs={{0,8},{1,9},{2,10},{3,11},{4,12},{5,13},{6,14},{7,15},{8,0},{9,1},... | collective-permute-start | bytes 405512 | tf_op jit(solution)/shard_map/ppermute | solution.py:339
where the time goes:
time: 27.4 us; the launch traced here: 27.3 us
  starting transfers between devices  12.3 us (45%)
  Pallas kernels  7.13 us (26%)
  waiting for transfers between devices  6.4 us (23%)
  other arithmetic  1.34 us (5%)
    ppermute x7, starting transfers between devices, steps(): moved = lax.ppermute(parts[hop], ('expo', 'sky'), pairs)  11.7 us
    pallas_call x5, Pallas kernels, call(): pl.pallas_call(body, out_shape=[jax.ShapeDtypeStruct(shape, jnp.float32)...  7.13 us
    ppermute x7, waiting for transfers between devices, steps(): moved = lax.ppermute(parts[hop], ('expo', 'sky'), pairs)  6.4 us
    another operation x2, other arithmetic, steps(): own = jnp.stack([science * weighted, weighted])  1.24 us
    ppermute x1, starting transfers between devices, steps(): other = lax.ppermute(own, 'sky', [(0, 1), (1, 0)])  0.56 us
  transfers between devices with their start and end apart: 8, of which 4 were waited for; matrix products, arithmetic and copies ran while one was open for 0% of the time, Pallas kernels for 15%

commit v1 on v0

--- a/solution.py
+++ b/solution.py
@@ -199,13 +199,7 @@
     stack_targets(outs, hops, wide, edge, offset_ref, shift_ref, sky, rows, chunks, lane)
 
 
-def rest_kernel(offset_ref, shift_ref, wide, edge, *outs, hops, rows, chunks):
-    sky = lax.axis_index("sky")
-    lane = lax.broadcasted_iota(jnp.int32, (SUB, LANES), 1)
-    stack_targets(outs, hops, wide, edge, offset_ref, shift_ref, sky, rows, chunks, lane)
-
-
-def last_kernel(offset_ref, shift_ref, trail_ref, wide, edge, trail_out, *outs, hops, rows, chunks):
+def rest_kernel(offset_ref, shift_ref, trail_ref, wide, edge, trail_out, *outs, hops, rows, chunks):
     sky = lax.axis_index("sky")
     lane = lax.broadcasted_iota(jnp.int32, (SUB, LANES), 1)
     taps = trail_ref.shape[0]
@@ -301,7 +295,7 @@
         functools.partial(near_kernel, rows=rows, chunks=chunks, taps=taps),
         [image_shape, wide_shape, spread_shape], [spread, (VMEM, own)],
     )
-    early, middle, late = stacking_order(count)
+    early, late = sending_order(count)
     results = call(
         functools.partial(far_kernel, hops=early, rows=rows, chunks=chunks, taps=taps),
         [image_shape, wide_shape, edge_shape] + [part] * len(early),
@@ -317,12 +311,7 @@
     wide, edge = results[1:3]
     parts = dict(zip(early, results[3:]))
     results = call(
-        functools.partial(rest_kernel, hops=middle, rows=rows, chunks=chunks),
-        [part] * len(middle), [offsets, shifts, (VMEM, wide), (VMEM, edge)],
-    )
-    parts.update(zip(middle, results))
-    results = call(
-        functools.partial(last_kernel, hops=late, rows=rows, chunks=chunks),
+        functools.partial(rest_kernel, hops=late, rows=rows, chunks=chunks),
         [(per, 2, trail_taps * trail_taps, SUB, LANES)] + [part] * len(late),
         [offsets, shifts, (SMEM, jnp.transpose(trail_kernel, (1, 0, 2))), (VMEM, wide), (VMEM, edge)],
     )
@@ -349,10 +338,10 @@
     )[0]
 
 
-def stacking_order(count):
-    early = [hop for hop in (count - 1, count - 3) if hop > 0]
-    middle = [hop for hop in (count - 2, count - 5) if hop > 0 and hop not in early]
-    return early, middle, [hop for hop in range(count - 1, -1, -1) if hop not in early + middle]
+def sending_order(count):
+    hops = list(range(count - 1, 0, -2)) + list(range(count - 2, -1, -2))
+    early = [hop for hop in (count - 1, count // 2 - 1) if hop > 0]
+    return early, [hop for hop in hops if hop not in early]
 
 
 def solution(mesh):

time: 27.4 us -> 27.9 us (1.018)
  waiting for transfers between devices: 6.4 us -> 8.43 us
  starting transfers between devices: 12.3 us -> 11.4 us
  Pallas kernels: 7.13 us -> 6.45 us
    ppermute x7, waiting for transfers between devices: 6.4 us -> 8.43 us  [steps(): moved = lax.ppermute(parts[hop], ('expo', 'sky'), pairs)]
    ppermute x7, starting transfers between devices: 11.7 us -> 10.9 us  [steps(): moved = lax.ppermute(parts[hop], ('expo', 'sky'), pairs)]
    pallas_call x5 -> x4, Pallas kernels: 7.13 us -> 6.45 us  [call(): pl.pallas_call(body, out_shape=[jax.ShapeDtypeStruct(shape, jnp.float32)...]
  transfers between devices with their start and end apart: 8 -> 8, of which waited for: 4 -> 3; matrix products, arithmetic and copies ran while one was open for 0% -> 0% of each run, Pallas kernels for 15% -> 12%
where the time goes in v1:
time: 27.9 us; the launch traced here: 27.8 us
  starting transfers between devices  11.4 us (41%)
  waiting for transfers between devices  8.43 us (30%)
  Pallas kernels  6.45 us (23%)
  other arithmetic  1.36 us (5%)
    ppermute x7, starting transfers between devices, steps(): moved = lax.ppermute(parts[hop], ('expo', 'sky'), pairs)  10.9 us
    ppermute x7, waiting for transfers between devices, steps(): moved = lax.ppermute(parts[hop], ('expo', 'sky'), pairs)  8.43 us
    pallas_call x4, Pallas kernels, call(): pl.pallas_call(body, out_shape=[jax.ShapeDtypeStruct(shape, jnp.float32)...  6.45 us
    another operation x2, other arithmetic, steps(): own = jnp.stack([science * weighted, weighted])  1.25 us
  transfers between devices with their start and end apart: 8, of which 3 were waited for; matrix products, arithmetic and copies ran while one was open for 0% of the time, Pallas kernels for 12%

profile of v1, /device:TPU:0, one launch (start us, length us, event | category | flops | bytes accessed | tf_op | source)
XLA Modules:
  0.0 27.8 jit_solution(1902868269790603437)
XLA Ops:
  0.0 0.0 copy-start
  0.0 0.0 copy-start.2
  0.0 0.0 copy-start.1
  0.0 1.2 %multiply_bitcast_fusion = (f32[1,4,32,512]{3,2,1,0:T(8,128)S(1)}, f32[1,4,32,512]{3,2,1,0:T(8,128)S(1)}) fusion(f32[4,32,512]{2,1,0:T(8,128)} %param.7, f32[4,32,512]{2,1,0:T(8,128)} %param.8, s32[4,32,512]{2,1,0:T(8,128)} %param.9), kind=kLoop, calls=%fused_computation.1 | loop fusion | flops 196608 | bytes 1310720 | tf_op jit(solution)/shard_map/stack | solution.py:282
  1.3 0.6 %collective-permute-start = (f32[2,4,32,512]{3,2,1,0:T(8,128)S(1)}, f32[2,4,32,512]{3,2,1,0:T(8,128)S(1)}, u32[]{:S(2)}, u32[]{:S(2)}) collective-permute-start(f32[2,4,32,512]{3,2,1,0:T(8,128)S(1)} %pad_maximum_fusion.own_ref), channel_id=1, source_target_pairs={{0,1},{1,0},{2,3},{3,2},{4,5},{5,4},{6,7},{7,6},{8,9},{9,8},{10,11... | collective-permute-start | bytes 1572872 | tf_op jit(solution)/shard_map/ppermute | solution.py:283
  1.8 0.0 copy-done
  1.8 1.5 %shard_map.73 = (f32[2,4,4,80,128]{4,3,2,1,0:T(8,128)S(1)}, f32[4,2,7,64,128]{4,3,2,1,0:T(8,128)S(1)}, f32[4,2,25,8,128]{4,3,2,1,0:T(8,128)S(1)}) custom-call(f32[5,4,5]{2,1,0:T(4,128)S(1)} %bitcast.8, f32[2,4,32,512]{3,2,1,0:T(8,128)S(1)} %pad_maximum_fusion.own_ref), custom_call_target="tpu_custom_call" | custom-call | tf_op jit(solution)/shard_map/pallas_call | solution.py:260
  3.4 0.0 collective-permute-done.other_ref
  3.4 0.0 copy-done.2
  3.4 0.0 copy-done.1
  3.4 0.0 copy-start.3
  3.4 2.3 %shard_map.74 = (f32[2,4,4,80,128]{4,3,2,1,0:T(8,128)S(1)}, f32[4,2,7,64,128]{4,3,2,1,0:T(8,128)S(1)}, f32[4,2,7,8,128]{4,3,2,1,0:T(8,128)S(1)}, f32[1,264,128]{2,1,0:T(8,128)S(1)}, f32[1,264,128]{2,1,0:T(8,128)S(1)}) custom-call(f32[4,2,25,8,128]{4,3,2,1,0:T(8,128)S(1)} %get-tuple-element.19.spread_ref, ...), custom_call_target="tpu_custom_call", output_to_operand_aliasing={{0}: (4, {}), {1}: (5, {})} | custom-call | tf_op jit(solution)/shard_map/pallas_call | solution.py:260
  5.7 2.9 %collective-permute-start.5 = (f32[1,264,128]{2,1,0:T(8,128)S(1)}, f32[1,264,128]{2,1,0:T(8,128)S(1)}, u32[]{:S(2)}, u32[]{:S(2)}) collective-permute-start(f32[1,264,128]{2,1,0:T(8,128)S(1)} %get-tuple-element.32), channel_id=1, source_target_pairs={{0,2},{1,5},{2,0},{3,7},{4,6},{5,1},{6,4},{7,3},{8,10},{9,13},{10,... | collective-permute-start | bytes 405512 | tf_op jit(solution)/shard_map/ppermute | solution.py:328
  8.6 0.1 collective-permute-start.2
  8.7 0.0 copy-done.3
  8.7 1.8 %shard_map.75 = (f32[1,2,9,8,128]{4,3,2,1,0:T(8,128)S(1)}, f32[1,264,128]{2,1,0:T(8,128)S(1)}, f32[1,264,128]{2,1,0:T(8,128)S(1)}, f32[1,264,128]{2,1,0:T(8,128)...) custom-call(s32[4,8]{1,0:T(4,128)S(1)} %bitcast.10, ...), custom_call_target="tpu_custom_call" | custom-call | tf_op jit(solution)/shard_map/pallas_call | solution.py:260
  10.5 2.0 %collective-permute-start.4 = (f32[1,264,128]{2,1,0:T(8,128)S(1)}, f32[1,264,128]{2,1,0:T(8,128)S(1)}, u32[]{:S(2)}, u32[]{:S(2)}) collective-permute-start(f32[1,264,128]{2,1,0:T(8,128)S(1)} %get-tuple-element.30), channel_id=1, source_target_pairs={{0,2},{1,5},{2,0},{3,7},{4,6},{5,1},{6,4},{7,3},{8,10},{9,13},{10,... | collective-permute-start | bytes 405512 | tf_op jit(solution)/shard_map/ppermute | solution.py:328
  12.5 0.0 collective-permute-done.5
  12.6 1.6 %collective-permute-start.6 = (f32[1,264,128]{2,1,0:T(8,128)S(1)}, f32[1,264,128]{2,1,0:T(8,128)S(1)}, u32[]{:S(2)}, u32[]{:S(2)}) collective-permute-start(f32[1,264,128]{2,1,0:T(8,128)S(1)} %add.25), channel_id=1, source_target_pairs={{0,4},{1,3},{2,6},{3,1},{4,0},{5,7},{6,2},{7,5},{8,12},{9,11},{10,... | collective-permute-start | bytes 405512 | tf_op jit(solution)/shard_map/ppermute | solution.py:328
  14.2 1.1 %collective-permute-start.1 = (f32[1,264,128]{2,1,0:T(8,128)S(1)}, f32[1,264,128]{2,1,0:T(8,128)S(1)}, u32[]{:S(2)}, u32[]{:S(2)}) collective-permute-start(f32[1,264,128]{2,1,0:T(8,128)S(1)} %get-tuple-element.26), channel_id=1, source_target_pairs={{0,2},{1,5},{2,0},{3,7},{4,6},{5,1},{6,4},{7,3},{8,10},{9,13},{10,... | collective-permute-start | bytes 405512 | tf_op jit(solution)/shard_map/ppermute | solution.py:328
  15.3 0.0 collective-permute-done.2
  15.3 0.5 %collective-permute-start.3 = (f32[1,264,128]{2,1,0:T(8,128)S(1)}, f32[1,264,128]{2,1,0:T(8,128)S(1)}, u32[]{:S(2)}, u32[]{:S(2)}) collective-permute-start(f32[1,264,128]{2,1,0:T(8,128)S(1)} %add.22), channel_id=1, source_target_pairs={{0,4},{1,3},{2,6},{3,1},{4,0},{5,7},{6,2},{7,5},{8,12},{9,11},{10,... | collective-permute-start | bytes 405512 | tf_op jit(solution)/shard_map/ppermute | solution.py:328
  15.8 0.8 %collective-permute-done.4 = f32[1,264,128]{2,1,0:T(8,128)S(1)} collective-permute-done((f32[1,264,128]{2,1,0:T(8,128)S(1)}, f32[1,264,128]{2,1,0:T(8,128)S(1)}, u32[]{:S(2)}, u32[]{:S(2)}) %collective-permute-start.4) | collective-permute-done | bytes 135200 | tf_op jit(solution)/shard_map/ppermute | solution.py:328
  16.6 2.1 %collective-permute-done.6 = f32[1,264,128]{2,1,0:T(8,128)S(1)} collective-permute-done((f32[1,264,128]{2,1,0:T(8,128)S(1)}, f32[1,264,128]{2,1,0:T(8,128)S(1)}, u32[]{:S(2)}, u32[]{:S(2)}) %collective-permute-start.6) | collective-permute-done | bytes 135200 | tf_op jit(solution)/shard_map/ppermute | solution.py:328
  18.7 2.7 %collective-permute-start.7 = (f32[1,264,128]{2,1,0:T(8,128)S(1)}, f32[1,264,128]{2,1,0:T(8,128)S(1)}, u32[]{:S(2)}, u32[]{:S(2)}) collective-permute-start(f32[1,264,128]{2,1,0:T(8,128)S(1)} %add_add_fusion), channel_id=1, source_target_pairs={{0,8},{1,9},{2,10},{3,11},{4,12},{5,13},{6,14},{7,15},{8,0},{9,1},... | collective-permute-start | bytes 405512 | tf_op jit(solution)/shard_map/ppermute | solution.py:328
  21.4 0.0 collective-permute-done.1
  21.4 0.0 collective-permute-done.3
  21.4 5.5 %collective-permute-done.7 = f32[1,264,128]{2,1,0:T(8,128)S(1)} collective-permute-done((f32[1,264,128]{2,1,0:T(8,128)S(1)}, f32[1,264,128]{2,1,0:T(8,128)S(1)}, u32[]{:S(2)}, u32[]{:S(2)}) %collective-permute-start.7) | collective-permute-done | bytes 135200 | tf_op jit(solution)/shard_map/ppermute | solution.py:328
  27.0 0.8 %shard_map.76 = f32[1,32,512]{2,1,0:T(8,128)} custom-call(f32[1,2,9,8,128]{4,3,2,1,0:T(8,128)S(1)} %get-tuple-element.24.trail_ref, f32[1,264,128]{2,1,0:T(8,128)S(1)} %add_add_fusion.1.rest_0_), custom_call_target="tpu_custom_call" | custom-call | tf_op jit(solution)/shard_map/pallas_call | solution.py:260
  (5 shorter events, 0.2 us)
Async XLA Ops:
  0.0 1.8 %copy-start = (f32[4,5,5]{2,0,1:T(4,128)S(1)}, f32[4,5,5]{2,0,1:T(4,128)}, u32[]{:S(2)}) copy-start(f32[4,5,5]{2,0,1:T(4,128)} %param.10) | copy-start | bytes 1204
  0.0 3.4 %copy-start.2 = (s32[8,4]{0,1:T(4,128)S(1)}, s32[8,4]{0,1:T(4,128)}, u32[]{:S(2)}) copy-start(s32[8,4]{0,1:T(4,128)} %param.12) | copy-start | bytes 388
  0.0 3.4 %copy-start.1 = (s32[8,4]{0,1:T(4,128)S(1)}, s32[8,4]{0,1:T(4,128)}, u32[]{:S(2)}) copy-start(s32[8,4]{0,1:T(4,128)} %param.11) | copy-start | bytes 388
  1.3 2.1 %collective-permute-start = (f32[2,4,32,512]{3,2,1,0:T(8,128)S(1)}, f32[2,4,32,512]{3,2,1,0:T(8,128)S(1)}, u32[]{:S(2)}, u32[]{:S(2)}) collective-permute-start(f32[2,4,32,512]{3,2,1,0:T(8,128)S(1)} %pad_maximum_fusion.own_ref), channel_id=1, source_target_pairs={{0,1},{1,0},{2,3},{3,2},{4,5},{5,4},{6,7},{7,6},{8,9},{9,8},{10,11... | collective-permute-start | bytes 1572872 | tf_op jit(solution)/shard_map/ppermute | solution.py:283
  3.4 5.3 %copy-start.3 = (f32[1,3,3]{2,0,1:T(1,128)S(1)}, f32[1,3,3]{2,0,1:T(1,128)}, u32[]{:S(2)}) copy-start(f32[1,3,3]{2,0,1:T(1,128)} %param.13) | copy-start | bytes 112
  5.7 6.8 %collective-permute-start.5 = (f32[1,264,128]{2,1,0:T(8,128)S(1)}, f32[1,264,128]{2,1,0:T(8,128)S(1)}, u32[]{:S(2)}, u32[]{:S(2)}) collective-permute-start(f32[1,264,128]{2,1,0:T(8,128)S(1)} %get-tuple-element.32), channel_id=1, source_target_pairs={{0,2},{1,5},{2,0},{3,7},{4,6},{5,1},{6,4},{7,3},{8,10},{9,13},{10,... | collective-permute-start | bytes 405512 | tf_op jit(solution)/shard_map/ppermute | solution.py:328
  8.6 6.7 %collective-permute-start.2 = (f32[1,264,128]{2,1,0:T(8,128)S(1)}, f32[1,264,128]{2,1,0:T(8,128)S(1)}, u32[]{:S(2)}, u32[]{:S(2)}) collective-permute-start(f32[1,264,128]{2,1,0:T(8,128)S(1)} %get-tuple-element.28), channel_id=1, source_target_pairs={{0,2},{1,5},{2,0},{3,7},{4,6},{5,1},{6,4},{7,3},{8,10},{9,13},{10,... | collective-permute-start | bytes 405512 | tf_op jit(solution)/shard_map/ppermute | solution.py:328
  10.5 6.1 %collective-permute-start.4 = (f32[1,264,128]{2,1,0:T(8,128)S(1)}, f32[1,264,128]{2,1,0:T(8,128)S(1)}, u32[]{:S(2)}, u32[]{:S(2)}) collective-permute-start(f32[1,264,128]{2,1,0:T(8,128)S(1)} %get-tuple-element.30), channel_id=1, source_target_pairs={{0,2},{1,5},{2,0},{3,7},{4,6},{5,1},{6,4},{7,3},{8,10},{9,13},{10,... | collective-permute-start | bytes 405512 | tf_op jit(solution)/shard_map/ppermute | solution.py:328
  12.6 6.2 %collective-permute-start.6 = (f32[1,264,128]{2,1,0:T(8,128)S(1)}, f32[1,264,128]{2,1,0:T(8,128)S(1)}, u32[]{:S(2)}, u32[]{:S(2)}) collective-permute-start(f32[1,264,128]{2,1,0:T(8,128)S(1)} %add.25), channel_id=1, source_target_pairs={{0,4},{1,3},{2,6},{3,1},{4,0},{5,7},{6,2},{7,5},{8,12},{9,11},{10,... | collective-permute-start | bytes 405512 | tf_op jit(solution)/shard_map/ppermute | solution.py:328
  14.2 7.2 %collective-permute-start.1 = (f32[1,264,128]{2,1,0:T(8,128)S(1)}, f32[1,264,128]{2,1,0:T(8,128)S(1)}, u32[]{:S(2)}, u32[]{:S(2)}) collective-permute-start(f32[1,264,128]{2,1,0:T(8,128)S(1)} %get-tuple-element.26), channel_id=1, source_target_pairs={{0,2},{1,5},{2,0},{3,7},{4,6},{5,1},{6,4},{7,3},{8,10},{9,13},{10,... | collective-permute-start | bytes 405512 | tf_op jit(solution)/shard_map/ppermute | solution.py:328
  15.3 6.1 %collective-permute-start.3 = (f32[1,264,128]{2,1,0:T(8,128)S(1)}, f32[1,264,128]{2,1,0:T(8,128)S(1)}, u32[]{:S(2)}, u32[]{:S(2)}) collective-permute-start(f32[1,264,128]{2,1,0:T(8,128)S(1)} %add.22), channel_id=1, source_target_pairs={{0,4},{1,3},{2,6},{3,1},{4,0},{5,7},{6,2},{7,5},{8,12},{9,11},{10,... | collective-permute-start | bytes 405512 | tf_op jit(solution)/shard_map/ppermute | solution.py:328
  18.7 8.2 %collective-permute-start.7 = (f32[1,264,128]{2,1,0:T(8,128)S(1)}, f32[1,264,128]{2,1,0:T(8,128)S(1)}, u32[]{:S(2)}, u32[]{:S(2)}) collective-permute-start(f32[1,264,128]{2,1,0:T(8,128)S(1)} %add_add_fusion), channel_id=1, source_target_pairs={{0,8},{1,9},{2,10},{3,11},{4,12},{5,13},{6,14},{7,15},{8,0},{9,1},... | collective-permute-start | bytes 405512 | tf_op jit(solution)/shard_map/ppermute | solution.py:328
